TPU v7x, 256 devices: a whole 4x4x8 slice. The times are simulated.
256 devices in a mesh: dp: 16 (over y, x_lo, core), fsdp: 16 (over z, x_hi).
Axes of the slice: x: 4 (x_hi: 2, x_lo: 2; x = x_hi * 2 + x_lo), y: 4, z: 8, core: 2. Of those that a mesh axis runs over, the one named last changes fastest.
Arguments:
- tokens: bfloat16 [2048, 5120], P('dp'), may hold values from -6 to 6
- targets: bfloat16 [2048, 5120], P('dp'), may hold values from -12 to 12
- norm_gain: float32 [5120], replicated, may hold values from 0.5 to 1.5
- up_master: float32 [5120, 6912], P('dp', 'fsdp'), may hold values from -0.078125 to 0.078125
- down_master: float32 [6912, 5120], P('fsdp', 'dp'), may hold values from -0.078125 to 0.078125
- up_probe: int32 [160, 6912], P(None, 'fsdp'), may hold values from -2147483648 to 2147483646
- down_probe: int32 [6912, 160], P('fsdp'), may hold values from -2147483648 to 2147483646
- up_first: float32 [5120, 6912], P('dp', 'fsdp'), may hold values from -0.012 to 0.012
- up_second: float32 [5120, 6912], P('dp', 'fsdp'), may hold values from 0.0001 to 0.001
- down_first: float32 [6912, 5120], P('fsdp', 'dp'), may hold values from -0.012 to 0.012
- down_second: float32 [6912, 5120], P('fsdp', 'dp'), may hold values from 0.0001 to 0.001
Outputs:
- loss: float32 [], replicated
- up_moment: float32 [5120, 6912], P('dp', 'fsdp')
- up_curvature: float32 [5120, 6912], P('dp', 'fsdp')
- up_step: float32 [5120, 6912], P('dp', 'fsdp')
- down_moment: float32 [6912, 5120], P('fsdp', 'dp')
- down_curvature: float32 [6912, 5120], P('fsdp', 'dp')
- down_step: float32 [6912, 5120], P('fsdp', 'dp')
Inputs may be any that keep to these rules, and one draw needn't show every extreme that they name: `up_probe`: any 32-bit word; each bit gives one probe sign. `down_probe`: any 32-bit word; each bit gives one probe sign.
All inputs are finite; a program needn't handle non-finite values.
Results may differ from a plain program's by a relative error of at most 0.03.
Values may be sent and summed in bfloat16 or wider, within the bound.
No kernel may reach another device: no remote copies, remote signals or barrier semaphores. Data moves between devices by JAX's collectives and lax.ppermute only.
A program may use at most 128 MiB of HBM per device.

v0:
```python
import jax
import jax.numpy as jnp
from jax import lax
from jax.sharding import Mesh, PartitionSpec as P

BLOCK = 16
STEP = 10
N_Z = 8
norm_eps = 1e-05
beta_one = 0.9
beta_two = 0.999
adam_eps = 1e-08
DP = ("y", "xlo", "core")
FS = ("z", "xhi")


def signs_rows(probe):
    shifts = jnp.arange(32, dtype=jnp.int32)[:, None, None]
    bits = jnp.bitwise_and(jnp.right_shift(probe[None, :, :], shifts), 1)
    return (1 - 2 * bits).reshape(32 * probe.shape[0], probe.shape[1]).astype(jnp.bfloat16)


def own_signs(probe, index):
    shifts = (2 * index + jnp.arange(2, dtype=jnp.int32))[:, None, None]
    bits = jnp.bitwise_and(jnp.right_shift(probe[None, :, :], shifts), 1)
    return (1 - 2 * bits).reshape(2 * probe.shape[0], probe.shape[1]).astype(jnp.float32)


def dot_last(left, right):
    return lax.dot_general(
        left, right, (((1,), (1,)), ((), ())), preferred_element_type=jnp.float32
    )


def dot_plain(left, right):
    return jnp.dot(left, right, preferred_element_type=jnp.float32)


def dot_first(left, right):
    return lax.dot_general(
        left, right, (((0,), (0,)), ((), ())), preferred_element_type=jnp.float32
    )


def gathered(shard, axis):
    return lax.all_gather(shard, axis, axis=0, tiled=True)


def sent_to_all(shard, axis):
    devices = lax.axis_size(axis)
    return lax.all_to_all(
        jnp.broadcast_to(shard[None], (devices, *shard.shape)), axis, 0, 0, tiled=True
    )


def after(value, other):
    return lax.optimization_barrier((value, other))[0]


def interleaved(first, second):
    rows, cols = first.shape
    parts = [v.reshape(N_Z, rows // N_Z, cols) for v in (first, second)]
    return jnp.stack(parts, axis=1).reshape(2 * rows, cols)


def apart(both):
    rows, cols = both.shape
    parts = both.reshape(N_Z, 2, rows // (2 * N_Z), cols)
    return (parts[:, 0].reshape(rows // 2, cols), parts[:, 1].reshape(rows // 2, cols))


def over_pairs(value):
    total = value
    for axis, pairs in (
        ("core", ((0, 1), (1, 0))),
        ("xlo", ((0, 1), (1, 0))),
        ("y", ((0, 1), (1, 0), (2, 3), (3, 2))),
        ("y", ((0, 2), (2, 0), (1, 3), (3, 1))),
    ):
        total = total + lax.ppermute(total, axis, pairs)
    return total


def stepped(grad, diag, first, second):
    first_new = beta_one * first + (1.0 - beta_one) * grad
    second_new = beta_two * second + (1.0 - beta_two) * diag * diag
    direction = (
        first_new
        / (1.0 - beta_one**STEP)
        / (jnp.sqrt(second_new / (1.0 - beta_two**STEP)) + adam_eps)
    )
    return (first_new, second_new, direction)


def local(
    tokens,
    targets,
    norm_gain,
    up_master,
    down_master,
    up_probe,
    down_probe,
    up_first,
    up_second,
    down_first,
    down_second,
):
    rows, width = tokens.shape
    own_rows, hidden = up_master.shape
    tokens_all = jnp.float32(rows * lax.axis_size(DP))
    index = lax.axis_index(DP)
    z = lax.axis_index("z")
    up_full = gathered(up_master.astype(jnp.bfloat16), DP)
    down_own = after(down_master.T.astype(jnp.bfloat16), up_full[:16, :128])
    down_full = gathered(down_own, DP)
    up_signs = signs_rows(up_probe)
    down_probe_t = down_probe.T
    down_signs = signs_rows(down_probe_t)
    values = tokens.astype(jnp.float32)
    scale = lax.rsqrt(jnp.mean(values * values, axis=-1, keepdims=True) + norm_eps)
    normed = (values * scale * norm_gain).astype(jnp.bfloat16)
    preact_dir = dot_plain(normed, up_signs)
    preact = dot_plain(normed, up_full)
    logistic = jax.nn.sigmoid(preact)
    active = (preact * logistic).astype(jnp.bfloat16)
    slopes = logistic * (1.0 + preact * (1.0 - logistic))
    curves = logistic * (1.0 - logistic) * (2.0 + preact * (1.0 - 2.0 * logistic))
    active_dir = (slopes * preact_dir).astype(jnp.bfloat16)
    acts = interleaved(active_dir, active)
    lead = interleaved(active, active_dir)
    side = interleaved(jnp.zeros_like(active), active)
    partial = dot_last(lead, down_full) + dot_last(side, down_signs)
    partial = partial.astype(jnp.bfloat16)
    scattered = lax.psum_scatter(partial, "z", scatter_dimension=0, tiled=True)
    acts_later, normed_later = lax.optimization_barrier((acts, normed, partial))[:2]
    acts_all = sent_to_all(acts_later, DP).reshape(-1, hidden)
    inputs = lax.all_to_all(normed_later, DP, split_axis=1, concat_axis=0, tiled=True)
    other = lax.ppermute(scattered, "xhi", ((0, 1), (1, 0)))
    total = scattered.astype(jnp.float32) + other.astype(jnp.float32)
    few = rows // N_Z
    goal = lax.dynamic_slice_in_dim(targets, z * few, few, 0).astype(jnp.float32)
    less = jnp.concatenate([goal, jnp.zeros_like(goal)], axis=0)
    own_res = ((total - less) / tokens_all).astype(jnp.bfloat16)
    res_both = gathered(own_res, "z")
    res_all = lax.all_to_all(res_both, DP, split_axis=1, concat_axis=0, tiled=True)
    residual, _ = apart(res_both)
    res32 = residual.astype(jnp.float32)
    loss = over_pairs(0.5 * jnp.sum(res32 * res32) * tokens_all)
    main = dot_plain(res_both, down_full)
    extra = dot_plain(res_both, down_signs)
    grad_active, hess_active = apart(main)
    hess_active = hess_active + apart(extra)[0]
    grad_preact = (slopes * grad_active).astype(jnp.bfloat16)
    hess_preact = (curves * preact_dir * grad_active + slopes * hess_active).astype(jnp.bfloat16)
    grads_all = gathered(jnp.stack([grad_preact, hess_preact])[None], DP)
    down_hess = dot_first(res_all, acts_all)
    blocks = acts_all.shape[0] // (2 * few)
    act_all = acts_all.reshape(blocks, 2, few, hidden)[:, 1].reshape(-1, hidden)
    resid_all = res_all.reshape(blocks, 2, few, own_rows)[:, 0].reshape(-1, own_rows)
    down_grad = dot_first(resid_all, act_all)
    up_grad = dot_first(inputs, grads_all[:, 0].reshape(-1, hidden))
    up_hess = dot_first(inputs, grads_all[:, 1].reshape(-1, hidden))
    up_hut = jnp.abs(own_signs(up_probe, index) * up_hess)
    spot = lax.broadcasted_iota(jnp.int32, (hidden, hidden), 0) // BLOCK
    place = lax.broadcasted_iota(jnp.int32, (hidden, hidden), 1) // BLOCK
    average = jnp.where(spot == place, 1.0 / BLOCK, 0.0).astype(jnp.float32)
    up_diag = jnp.dot(up_hut, average, precision=lax.Precision.HIGHEST)
    down_hut = jnp.abs(own_signs(down_probe_t, index) * down_hess)
    means = jnp.mean(down_hut.reshape(own_rows // BLOCK, BLOCK, hidden), axis=1)
    down_diag = jnp.repeat(means, BLOCK, axis=0)
    up_out = stepped(up_grad, up_diag, up_first, up_second)
    down_out = stepped(down_grad, down_diag, down_first.T, down_second.T)
    return (loss, *up_out, *(v.T for v in down_out))


def solution(mesh):
    fine = Mesh(mesh.devices.reshape(4, 2, 2, N_Z, 2), (*DP, *FS))
    placed = (
        P(DP, None),
        P(DP, None),
        P(),
        P(DP, FS),
        P(FS, DP),
        P(None, FS),
        P(FS, None),
        P(DP, FS),
        P(DP, FS),
        P(FS, DP),
        P(FS, DP),
    )
    return jax.shard_map(
        local,
        mesh=fine,
        in_specs=placed,
        out_specs=(P(), P(DP, FS), P(DP, FS), P(DP, FS), P(FS, DP), P(FS, DP), P(FS, DP)),
        check_vma=False,
    )
```

profile of v0, /device:TPU:1, one launch (start us, length us, event | category | flops | bytes accessed | tf_op | source)
XLA Modules:
  0.0 328.9 jit_solution(15331444754146490073)
XLA Ops:
  7.2 2.0 convert_element_type.71
  9.2 0.0 all-gather.8.cloned.1.call-start
  9.3 1.9 convert_bitcast_fusion
  11.2 0.0 reduce-scatter.2.cloned.1.call-start
  11.2 1.8 copy.106
  13.0 0.1 shift_right_arithmetic.82
  13.1 1.9 fusion.3
  15.1 0.7 fusion.5
  15.8 4.2 %subtract_convert_fusion = bf16[32,160,432]{2,1,0:T(8,128)(2,1)} fusion(s32[160,432]{1,0:T(8,128)S(1)} %bitcast.181), kind=kLoop, calls=%fused_computation.5 | loop fusion | flops 11059200 | bytes 4700160 | tf_op jit(solution)/shard_map/convert_element_type | solution.py:20
  20.0 3.0 fusion.7
  23.0 3.3 %fusion.97 = f32[128,432]{0,1:T(8,128)S(1)} fusion(bf16[128,5120]{0,1:T(8,128)(2,1)} %fusion.7, bf16[5120,432]{1,0:T(8,128)(2,1)S(1)} %fusion.3), kind=kOutput, calls=%fused_computation.104 | convolution fusion | flops 566231040 | bytes 5955584 | tf_op jit(solution)/shard_map/dot_general | solution.py:36
  26.4 29.9 %all-gather.6.cloned.1.call-done = bf16[5120,432]{1,0:T(8,128)(2,1)} async-done(((bf16[320,432]{1,0:T(8,128)(2,1)}), bf16[5120,432]{1,0:T(8,128)(2,1)}) %all-gather.6.cloned.1.call-update) | async-done | bytes 4423696 | tf_op jit(solution)/shard_map/all_gather | solution.py:46
  56.3 4.9 %multiply_convert_fusion.3 = (bf16[128,432]{0,1:T(8,128)(2,1)S(1)}, bf16[128,432]{0,1:T(8,128)(2,1)S(1)}, f32[128,432]{0,1:T(8,128)S(1)}) fusion(f32[128,432]{0,1:T(8,128)S(1)} %fusion.97, bf16[128,5120]{0,1:T(8,128)(2,1)} %fusion.7, bf16[5120,432]{1,0:T(8,128)(2,1)} %all-gather.6.cloned.1.call-done), kind=kOutput, calls=%fused_computation.85 | convolution fusion | flops 566839296 | bytes 6397952 | tf_op jit(solution)/shard_map/dot_general | solution.py:36
  61.2 0.1 copy.107
  61.3 0.1 copy.108
  61.6 39.2 %all-gather.8.cloned.1.call-done = bf16[5120,432]{1,0:T(8,128)(2,1)} async-done(((bf16[320,432]{1,0:T(8,128)(2,1)}), bf16[5120,432]{1,0:T(8,128)(2,1)}) %all-gather.8.cloned.1.call-update) | async-done | bytes 4423696 | tf_op jit(solution)/shard_map/all_gather | solution.py:46
  100.8 4.2 %fusion.98 = f32[256,5120]{1,0:T(8,128)S(1)} fusion(bf16[256,432]{1,0:T(8,128)(2,1)S(1)} %bitcast.189, bf16[5120,432]{1,0:T(8,128)(2,1)} %all-gather.8.cloned.1.call-done), kind=kOutput, calls=%fused_computation.105 | convolution fusion | flops 1132462080 | bytes 9887744 | tf_op jit(solution)/shard_map/dot_general | solution.py:30
  105.0 3.0 fusion.4
  108.1 40.1 %reduce-scatter.2.cloned.1.call-done = bf16[32,5120]{1,0:T(8,128)(2,1)} async-done(((bf16[256,5120]{1,0:T(8,128)(2,1)}), bf16[32,5120]{1,0:T(8,128)(2,1)}) %reduce-scatter.2.cloned.1.call-update) | async-done | bytes 327696 | tf_op jit(solution)/shard_map/reduce_scatter | solution.py:134
  148.2 2.7 collective-permute-start
  150.9 4.9 %collective-permute-done = bf16[32,5120]{1,0:T(8,128)(2,1)S(1)} collective-permute-done((bf16[32,5120]{1,0:T(8,128)(2,1)}, bf16[32,5120]{1,0:T(8,128)(2,1)S(1)}, u32[]{:S(2)}, u32[]{:S(2)}) %collective-permute-start) | collective-permute-done | bytes 327712 | tf_op jit(solution)/shard_map/ppermute | solution.py:138
  155.8 1.8 multiply_convert_fusion
  157.7 0.1 copy.123
  157.9 2.0 broadcast_in_dim.15
  159.9 11.1 %all-to-all-start.2 = ((bf16[16,256,432]{1,2,0:T(8,128)(2,1)}), bf16[16,256,432]{1,2,0:T(8,128)(2,1)}, u32[]{:S(2)}, u32[]{:S(2)}) async-start(bf16[16,256,432]{1,2,0:T(8,128)(2,1)} %broadcast_in_dim.15), calls=%async_computation.3 | async-start | bytes 7077888 | tf_op jit(solution)/shard_map/all_to_all | solution.py:51
  171.0 30.5 %all-gather.10.cloned.1.call-done = bf16[256,5120]{1,0:T(8,128)(2,1)} async-done(((bf16[32,5120]{1,0:T(8,128)(2,1)}), bf16[256,5120]{1,0:T(8,128)(2,1)}) %all-gather.10.cloned.1.call-update) | async-done | bytes 2621456 | tf_op jit(solution)/shard_map/all_gather | solution.py:46
  201.5 4.8 %fusion.99 = f32[256,432]{1,0:T(8,128)S(1)} fusion(bf16[256,5120]{1,0:T(8,128)(2,1)} %all-gather.10.cloned.1.call-done, bf16[5120,432]{1,0:T(8,128)(2,1)} %all-gather.8.cloned.1.call-done), kind=kOutput, calls=%fused_computation.106 | convolution fusion | flops 1132462080 | bytes 7487488 | tf_op jit(solution)/shard_map/dot_general | solution.py:36
  206.3 0.1 copy.114
  206.5 3.8 %convolution_add_fusion.1 = f32[8,1,16,432]{3,2,1,0:T(8,128)S(1)} fusion(bf16[8,2,16,5120]{3,2,1,0:T(8,128)(2,1)} %bitcast.173, bf16[5120,432,1,1]{1,0,3,2:T(8,128)(2,1)} %bitcast.169, f32[8,2,16,432]{3,2,1,0:T(8,128)S(1)} %bitcast.193), kind=kOutput, calls=%fused_computation.34 | convolution fusion | flops 566286336 | bytes 7487488 | tf_op jit(solution)/shard_map/slice | solution.py:69
  210.2 0.1 copy.117
  210.3 0.2 fusion.87
  210.5 0.7 pad_maximum_fusion.2
  211.3 4.4 %copy.120 = bf16[256,5120]{0,1:T(8,128)(2,1)} copy(bf16[256,5120]{1,0:T(8,128)(2,1)} %all-gather.10.cloned.1.call-done) | data formatting | bytes 5242880 | tf_op jit(solution)/shard_map/all_gather | solution.py:46
  215.7 9.0 %all-to-all-start.1 = ((bf16[256,16,320]{0,2,1:T(8,128)(2,1)}), bf16[256,16,320]{0,2,1:T(8,128)(2,1)}, u32[]{:S(2)}, u32[]{:S(2)}) async-start(bf16[256,16,320]{0,2,1:T(8,128)(2,1)} %bitcast.175), calls=%async_computation.2 | async-start | bytes 5242880 | tf_op jit(solution)/shard_map/all_to_all | solution.py:145
  224.7 0.1 shift_right_arithmetic.90
  224.8 0.1 shift_right_arithmetic.91
  224.9 1.3 fusion.67
  226.2 6.1 %copy.124 = bf16[16,256,432]{2,1,0:T(8,128)(2,1)} copy(bf16[16,256,432]{1,2,0:T(8,128)(2,1)} %all-to-all-done.2) | data formatting | bytes 7077888 | tf_op jit(solution)/shard_map/all_to_all | solution.py:51
  232.3 1.8 slice.39
  234.1 3.0 copy.132
  237.1 2.6 multiply_reduce_fusion
  240.4 1.1 collective-permute-start.1
  241.5 0.1 collective-permute-done.1
  242.3 20.7 %collective-permute-start.2 = (f32[]{:T(128)}, f32[]{:T(128)}, u32[]{:S(2)}, u32[]{:S(2)}) collective-permute-start(f32[]{:T(128)} %add.106), channel_id=1, source_target_pairs={{0,32},{32,0},{1,33},{33,1},{2,34},{34,2},{3,35},{35,3},{4,36},{36... | collective-permute-start | bytes 20 | tf_op jit(solution)/shard_map/ppermute | solution.py:80
  263.0 3.6 %collective-permute-done.2 = f32[]{:T(128)} collective-permute-done((f32[]{:T(128)}, f32[]{:T(128)}, u32[]{:S(2)}, u32[]{:S(2)}) %collective-permute-start.2) | collective-permute-done | bytes 36 | tf_op jit(solution)/shard_map/ppermute | solution.py:80
  267.3 0.8 collective-permute-start.3
  268.1 2.1 collective-permute-done.3
  270.9 10.6 %collective-permute-start.4 = (f32[]{:T(128)}, f32[]{:T(128)}, u32[]{:S(2)}, u32[]{:S(2)}) collective-permute-start(f32[]{:T(128)} %add.108), channel_id=1, source_target_pairs={{0,128},{128,0},{64,192},{192,64},{1,129},{129,1},{65,193},{193,65... | collective-permute-start | bytes 20 | tf_op jit(solution)/shard_map/ppermute | solution.py:80
  281.5 0.3 collective-permute-done.4
  282.6 7.4 %all-to-all-start = ((bf16[128,16,320]{0,2,1:T(8,128)(2,1)}), bf16[128,16,320]{0,2,1:T(8,128)(2,1)}, u32[]{:S(2)}, u32[]{:S(2)}) async-start(bf16[128,16,320]{0,2,1:T(8,128)(2,1)} %bitcast.10), calls=%async_computation.1 | async-start | bytes 2621440 | tf_op jit(solution)/shard_map/all_to_all | solution.py:137
  290.0 4.5 %copy.121 = bf16[16,256,320]{2,1,0:T(8,128)(2,1)} copy(bf16[16,256,320]{1,2,0:T(8,128)(2,1)} %bitcast.21) | data formatting | bytes 5242880 | tf_op jit(solution)/shard_map/all_to_all | solution.py:145
  294.5 1.6 slice.38
  296.1 1.1 copy.131
  297.2 5.4 %fusion.25 = f32[320,432]{1,0:T(8,128)} fusion(f32[320,432]{1,0:T(8,128)} %get-tuple-element.21, bf16[16,256,432]{1,2,0:T(8,128)(2,1)} %all-to-all-done.2, bf16[256,16,320]{0,2,1:T(8,128)(2,1)} %all-to-all-done.1), kind=kOutput, calls=%fused_computation.28 | convolution fusion | flops 1132738560 | bytes 7266304 | tf_op jit(solution)/shard_map/dot_general | solution.py:40
  302.7 1.2 reduce_sum.29
  303.9 2.9 bitcast_add_fusion.1
  306.8 1.4 fusion.63
  308.2 2.2 fusion.96
  310.5 1.7 copy.129
  312.1 0.5 copy.130
  312.6 0.6 copy-done.9
  313.2 2.8 fusion.46
  316.1 2.4 fusion.41
  318.5 2.7 add_divide_fusion
  (52 shorter events, 0.5 us)
Async XLA Ops:
  7.2 143.7 %copy-start = (bf16[128,5120]{1,0:T(8,128)(2,1)S(1)}, bf16[128,5120]{1,0:T(8,128)(2,1)}, u32[]{:S(2)}) copy-start(bf16[128,5120]{1,0:T(8,128)(2,1)} %param.12) | copy-start | bytes 3932164
  7.2 5.9 %copy-start.4 = (s32[160,432]{1,0:T(8,128)S(1)}, s32[160,432]{1,0:T(8,128)}, u32[]{:S(2)}) copy-start(s32[160,432]{1,0:T(8,128)} %param.16) | copy-start | bytes 829444
  7.2 49.1 %all-gather.6.cloned.1.call-start = ((), (), s32[]{:S(2)}) async-start(), calls=%async_computation.4 | async-start | bytes 5570560 | tf_op jit(solution)/shard_map/all_gather | solution.py:46
  9.2 91.5 %all-gather.8.cloned.1.call-start = ((), (), s32[]{:S(2)}) async-start(), calls=%async_computation.5 | async-start | bytes 5570560 | tf_op jit(solution)/shard_map/all_gather | solution.py:46
  11.2 137.0 %reduce-scatter.2.cloned.1.call-start = ((), (), s32[]{:S(2)}) async-start(), calls=%async_computation.6 | async-start | bytes 2949120 | tf_op jit(solution)/shard_map/reduce_scatter | solution.py:134
  13.1 2.7 copy-start.5
  15.8 4.2 %copy-start.8 = (f32[5120]{0:T(1024)S(1)}, f32[5120]{0:T(1024)}, u32[]{:S(2)}) copy-start(f32[5120]{0:T(1024)} %param.13) | copy-start | bytes 61444
  100.8 4.2 %slice-start = ((s8[5242880]{0:T(1024)(128)(4,1)}), s8[4194304]{0:T(1024)(128)(4,1)S(1)}, s32[]{:S(2)}) async-start(s8[5242880]{0:T(1024)(128)(4,1)} %bitcast.170), calls=%async_computation.9 | async-start | bytes 8388608
  100.8 4.2 %slice-start.1 = ((s8[5242880]{0:T(1024)(128)(4,1)}), s8[1048576]{0:T(1024)(128)(4,1)S(1)}, s32[]{:S(2)}) async-start(s8[5242880]{0:T(1024)(128)(4,1)} %bitcast.170), calls=%async_computation.10 | async-start | bytes 2097152
  108.0 93.5 %all-gather.10.cloned.1.call-start = ((), (), s32[]{:S(2)}) async-start(), calls=%async_computation.7 | async-start | bytes 2949120 | tf_op jit(solution)/shard_map/all_gather | solution.py:46
  148.2 7.6 %collective-permute-start = (bf16[32,5120]{1,0:T(8,128)(2,1)}, bf16[32,5120]{1,0:T(8,128)(2,1)S(1)}, u32[]{:S(2)}, u32[]{:S(2)}) collective-permute-start(bf16[32,5120]{1,0:T(8,128)(2,1)} %reduce-scatter.2.cloned.1.call-done), channel_id=1, source_target_pairs={{0,1},{1,0},{2,3},{3,2},{4,5},{5,4},{6,7},{7,6},{8,9},{9,8},{10,11... | collective-permute-start | bytes 983048 | tf_op jit(solution)/shard_map/ppermute | solution.py:138
  159.9 55.8 %all-to-all-start.2 = ((bf16[16,256,432]{1,2,0:T(8,128)(2,1)}), bf16[16,256,432]{1,2,0:T(8,128)(2,1)}, u32[]{:S(2)}, u32[]{:S(2)}) async-start(bf16[16,256,432]{1,2,0:T(8,128)(2,1)} %broadcast_in_dim.15), calls=%async_computation.3 | async-start | bytes 7077888 | tf_op jit(solution)/shard_map/all_to_all | solution.py:51
  171.0 137.2 %all-gather.12.cloned.1.call-start = ((), (), s32[]{:S(2)}) async-start(), calls=%async_computation.8 | async-start | bytes 3760128 | tf_op jit(solution)/shard_map/all_gather | solution.py:46
  215.7 66.9 %all-to-all-start.1 = ((bf16[256,16,320]{0,2,1:T(8,128)(2,1)}), bf16[256,16,320]{0,2,1:T(8,128)(2,1)}, u32[]{:S(2)}, u32[]{:S(2)}) async-start(bf16[256,16,320]{0,2,1:T(8,128)(2,1)} %bitcast.175), calls=%async_computation.2 | async-start | bytes 5242880 | tf_op jit(solution)/shard_map/all_to_all | solution.py:145
  240.4 1.2 collective-permute-start.1
  242.3 24.3 %collective-permute-start.2 = (f32[]{:T(128)}, f32[]{:T(128)}, u32[]{:S(2)}, u32[]{:S(2)}) collective-permute-start(f32[]{:T(128)} %add.106), channel_id=1, source_target_pairs={{0,32},{32,0},{1,33},{33,1},{2,34},{34,2},{3,35},{35,3},{4,36},{36... | collective-permute-start | bytes 20 | tf_op jit(solution)/shard_map/ppermute | solution.py:80
  267.3 2.9 collective-permute-start.3
  270.9 10.9 %collective-permute-start.4 = (f32[]{:T(128)}, f32[]{:T(128)}, u32[]{:S(2)}, u32[]{:S(2)}) collective-permute-start(f32[]{:T(128)} %add.108), channel_id=1, source_target_pairs={{0,128},{128,0},{64,192},{192,64},{1,129},{129,1},{65,193},{193,65... | collective-permute-start | bytes 20 | tf_op jit(solution)/shard_map/ppermute | solution.py:80
  282.6 30.0 %all-to-all-start = ((bf16[128,16,320]{0,2,1:T(8,128)(2,1)}), bf16[128,16,320]{0,2,1:T(8,128)(2,1)}, u32[]{:S(2)}, u32[]{:S(2)}) async-start(bf16[128,16,320]{0,2,1:T(8,128)(2,1)} %bitcast.10), calls=%async_computation.1 | async-start | bytes 2621440 | tf_op jit(solution)/shard_map/all_to_all | solution.py:137
  297.2 6.7 %copy-start.2 = (bf16[128,1,16,432]{0,3,2,1:T(8,128)(2,1)S(1)}, bf16[128,1,16,432]{0,3,2,1:T(8,128)(2,1)}, u32[]{:S(2)}) copy-start(bf16[128,1,16,432]{0,3,2,1:T(8,128)(2,1)} %copy.132) | copy-start | bytes 5308420
  303.9 2.9 copy-start.3
  303.9 2.9 copy-start.6
  312.1 1.1 copy-start.9
  313.2 2.8 copy-start.7
  316.0 2.5 copy-start.11
  316.1 2.5 copy-start.10
  318.5 2.8 copy-start.1
Sparse Core Ops, SparseCore 0:
  10.4 45.8 all-gather.5
  58.7 41.9 all-gather.7
  108.2 39.9 reduce-scatter.1
  157.8 43.6 all-gather.9
  211.4 67.6 all-gather.11
where the time goes:
time: 330 us; the launch traced here: 329 us
  waiting for transfers between devices  151 us (46%)
  starting transfers between devices  63.7 us (19%)
  matrix products  40.3 us (12%)
  local copies, waits for them, and re-layouts  32.3 us (10%)
  other arithmetic  23 us (7%)
  between operations  18.7 us (6%)
    all_gather x4, waiting for transfers between devices, gathered(): return lax.all_gather(shard, axis, axis=0, tiled=True)  99.6 us
    reduce_scatter x1, waiting for transfers between devices, local(): scattered = lax.psum_scatter(partial, 'z', scatter_dimension=0, tiled=True)  40.1 us
    ppermute x4, starting transfers between devices, over_pairs(): total = total + lax.ppermute(total, axis, pairs)  33.2 us
    dot_general x4, matrix products, dot_first(): lax.dot_general(left, right, (((0,), (0,)), ((), ())), preferred_element_...  13.5 us
    dot_general x3, matrix products, dot_plain(): return jnp.dot(left, right, preferred_element_type=jnp.float32)  13.1 us
    all_to_all x1, starting transfers between devices, sent_to_all(): lax.all_to_all(jnp.broadcast_to(shard[None], (devices, *shard.shape)), ax...  11.1 us
    all_to_all x1, starting transfers between devices, local(): lax.all_to_all(res_both, DP, split_axis=1, concat_axis=0, tiled=True)  9.05 us
    unnamed x33, local copies, waits for them, and re-layouts  8.69 us
  transfers between devices with their start and end apart: 13, of which 9 were waited for; matrix products, arithmetic and copies ran while one was open for 23% of the time, Pallas kernels for 0%

commit v1 on v0

--- a/solution.py
+++ b/solution.py
@@ -43,7 +43,16 @@
 
 
 def gathered(shard, axis):
-    return lax.all_gather(shard, axis, axis=0, tiled=True)
+
+    def start_lines(xs, dim_no=0):
+        return jnp.concatenate(
+            jax.lax.all_to_all(
+                jnp.stack(tuple((xs for _ in range(jax.lax.psum(1, axis)))), axis=0), axis, 0, 0
+            ),
+            axis=dim_no,
+        )
+
+    return start_lines(shard)
 
 
 def sent_to_all(shard, axis):

time: 330 us -> 472 us (1.43)
  waiting for transfers between devices: 151 us -> 265 us
  local copies, waits for them, and re-layouts: 32.3 us -> 47.8 us
  starting transfers between devices: 63.7 us -> 78.7 us
    all_to_all x0 -> x4, waiting for transfers between devices: none -> 157 us  [start_lines(): jax.lax.all_to_all(jnp.stack(tuple((xs for _ in range(jax.lax.psum(1, axi...]
    all_gather x4 -> x0, waiting for transfers between devices: 99.6 us -> none  [gathered(): return lax.all_gather(shard, axis, axis=0, tiled=True)]
    all_to_all x1, waiting for transfers between devices: 0.01 us -> 31.7 us  [sent_to_all(): lax.all_to_all(jnp.broadcast_to(shard[None], (devices, *shard.shape)), ax...]
    all_to_all x1, waiting for transfers between devices: 0.01 us -> 23.7 us  [local(): lax.all_to_all(res_both, DP, split_axis=1, concat_axis=0, tiled=True)]
    all_to_all x0 -> x4, starting transfers between devices: none -> 22.7 us  [start_lines(): jax.lax.all_to_all(jnp.stack(tuple((xs for _ in range(jax.lax.psum(1, axi...]
    all_to_all x1 -> x3, local copies, waits for them, and re-layouts: 4.54 us -> 15.4 us  [local(): lax.all_to_all(res_both, DP, split_axis=1, concat_axis=0, tiled=True)]
    another operation x0 -> x4, local copies, waits for them, and re-layouts: none -> 9.71 us  [start_lines(): jnp.stack(tuple((xs for _ in range(jax.lax.psum(1, axis)))), axis=0)]
    ppermute x4, starting transfers between devices: 33.2 us -> 27.6 us  [over_pairs(): total = total + lax.ppermute(total, axis, pairs)]
  transfers between devices with their start and end apart: 13 -> 13, of which waited for: 9 -> 12; matrix products, arithmetic and copies ran while one was open for 23% -> 15% of each run, Pallas kernels for 0% -> 0%
where the time goes in v1:
time: 472 us; the launch traced here: 470 us
  waiting for transfers between devices  265 us (56%)
  starting transfers between devices  78.7 us (17%)
  local copies, waits for them, and re-layouts  47.8 us (10%)
  matrix products  40.4 us (9%)
  other arithmetic  19.1 us (4%)
  between operations  18.7 us (4%)
    all_to_all x4, waiting for transfers between devices, start_lines(): jax.lax.all_to_all(jnp.stack(tuple((xs for _ in range(jax.lax.psum(1, axi...  157 us
    reduce_scatter x1, waiting for transfers between devices, local(): scattered = lax.psum_scatter(partial, 'z', scatter_dimension=0, tiled=True)  40.7 us
    all_to_all x1, waiting for transfers between devices, sent_to_all(): lax.all_to_all(jnp.broadcast_to(shard[None], (devices, *shard.shape)), ax...  31.7 us
    ppermute x4, starting transfers between devices, over_pairs(): total = total + lax.ppermute(total, axis, pairs)  27.6 us
    all_to_all x1, waiting for transfers between devices, local(): lax.all_to_all(res_both, DP, split_axis=1, concat_axis=0, tiled=True)  23.7 us
    all_to_all x4, starting transfers between devices, start_lines(): jax.lax.all_to_all(jnp.stack(tuple((xs for _ in range(jax.lax.psum(1, axi...  22.7 us
    all_to_all x3, local copies, waits for them, and re-layouts, local(): lax.all_to_all(res_both, DP, split_axis=1, concat_axis=0, tiled=True)  15.4 us
    dot_general x4, matrix products, dot_first(): lax.dot_general(left, right, (((0,), (0,)), ((), ())), preferred_element_...  13.5 us
  transfers between devices with their start and end apart: 13, of which 12 were waited for; matrix products, arithmetic and copies ran while one was open for 15% of the time, Pallas kernels for 0%

profile of v1, /device:TPU:1, one launch (start us, length us, event | category | flops | bytes accessed | tf_op | source)
XLA Modules:
  0.0 470.1 jit_solution(6569844224370361344)
XLA Ops:
  7.2 1.2 convert_element_type.71
  8.4 2.8 stack.20
  11.3 7.7 %all-to-all-start = ((bf16[16,320,432]{2,1,0:T(8,128)(2,1)}), bf16[16,320,432]{2,1,0:T(8,128)(2,1)}, u32[]{:S(2)}, u32[]{:S(2)}) async-start(bf16[16,320,432]{2,1,0:T(8,128)(2,1)} %stack.20), calls=%async_computation | async-start | bytes 10485760 | tf_op jit(solution)/shard_map/all_to_all | solution.py:49
  19.0 60.8 %all-to-all-done = bf16[16,320,432]{2,1,0:T(8,128)(2,1)} async-done(((bf16[16,320,432]{2,1,0:T(8,128)(2,1)}), bf16[16,320,432]{2,1,0:T(8,128)(2,1)}, u32[]{:S(2)}, u32[]{:S(2)}) %all-to-all-start) | async-done | bytes 4423712 | tf_op jit(solution)/shard_map/all_to_all | solution.py:49
  79.8 2.8 stack.22
  82.6 5.3 %all-to-all-start.1 = ((bf16[16,320,432]{2,1,0:T(8,128)(2,1)}), bf16[16,320,432]{2,1,0:T(8,128)(2,1)}, u32[]{:S(2)}, u32[]{:S(2)}) async-start(bf16[16,320,432]{2,1,0:T(8,128)(2,1)} %stack.22), calls=%async_computation.1 | async-start | bytes 10485760 | tf_op jit(solution)/shard_map/all_to_all | solution.py:49
  87.9 1.8 copy.124
  89.8 1.9 fusion.3
  91.8 0.7 fusion.5
  92.5 4.2 subtract_convert_fusion
  96.7 3.0 fusion.7
  99.7 3.3 fusion.97
  103.1 4.9 %multiply_convert_fusion.3 = (bf16[128,432]{0,1:T(8,128)(2,1)S(1)}, bf16[128,432]{0,1:T(8,128)(2,1)S(1)}, f32[128,432]{0,1:T(8,128)S(1)}) fusion(f32[128,432]{0,1:T(8,128)S(1)} %fusion.97, bf16[128,5120]{0,1:T(8,128)(2,1)} %fusion.7, bf16[5120,432]{1,0:T(8,128)(2,1)} %bitcast), kind=kOutput, calls=%fused_computation.85 | convolution fusion | flops 566839296 | bytes 6397952 | tf_op jit(solution)/shard_map/dot_general | solution.py:36
  108.3 40.4 %all-to-all-done.1 = bf16[16,320,432]{2,1,0:T(8,128)(2,1)} async-done(((bf16[16,320,432]{2,1,0:T(8,128)(2,1)}), bf16[16,320,432]{2,1,0:T(8,128)(2,1)}, u32[]{:S(2)}, u32[]{:S(2)}) %all-to-all-start.1) | async-done | bytes 4423712 | tf_op jit(solution)/shard_map/all_to_all | solution.py:49
  148.7 4.2 fusion.98
  152.9 3.1 fusion.4
  156.1 40.7 %reduce-scatter.2.cloned.1.call-done = bf16[32,5120]{1,0:T(8,128)(2,1)} async-done(((bf16[256,5120]{1,0:T(8,128)(2,1)}), bf16[32,5120]{1,0:T(8,128)(2,1)}) %reduce-scatter.2.cloned.1.call-update) | async-done | bytes 327696 | tf_op jit(solution)/shard_map/reduce_scatter | solution.py:143
  196.8 2.7 collective-permute-start
  199.5 4.9 %collective-permute-done = bf16[32,5120]{1,0:T(8,128)(2,1)S(1)} collective-permute-done((bf16[32,5120]{1,0:T(8,128)(2,1)}, bf16[32,5120]{1,0:T(8,128)(2,1)S(1)}, u32[]{:S(2)}, u32[]{:S(2)}) %collective-permute-start) | collective-permute-done | bytes 327712 | tf_op jit(solution)/shard_map/ppermute | solution.py:147
  204.4 1.1 multiply_convert_fusion
  205.5 1.9 stack.24
  207.4 4.6 all-to-all-start.2
  212.0 0.1 copy.141
  212.2 56.1 %all-to-all-done.2 = bf16[8,32,5120]{2,1,0:T(8,128)(2,1)} async-done(((bf16[8,32,5120]{2,1,0:T(8,128)(2,1)}), bf16[8,32,5120]{2,1,0:T(8,128)(2,1)}, u32[]{:S(2)}, u32[]{:S(2)}) %all-to-all-start.2) | async-done | bytes 2621472 | tf_op jit(solution)/shard_map/all_to_all | solution.py:49
  268.3 2.0 broadcast_in_dim.12
  270.3 12.6 %all-to-all-start.6 = ((bf16[16,256,432]{1,2,0:T(8,128)(2,1)}), bf16[16,256,432]{1,2,0:T(8,128)(2,1)}, u32[]{:S(2)}, u32[]{:S(2)}) async-start(bf16[16,256,432]{1,2,0:T(8,128)(2,1)} %broadcast_in_dim.12), calls=%async_computation.7 | async-start | bytes 7077888 | tf_op jit(solution)/shard_map/all_to_all | solution.py:60
  282.9 6.0 %all_to_all.49 = bf16[256,16,320]{2,1,0:T(8,128)(2,1)} reshape(bf16[8,32,5120]{2,1,0:T(8,128)(2,1)} %all-to-all-done.2) | data formatting | bytes 5242880 | tf_op jit(solution)/shard_map/all_to_all | solution.py:154
  288.8 4.9 %copy.138 = bf16[256,16,320]{0,2,1:T(8,128)(2,1)} copy(bf16[256,16,320]{2,1,0:T(8,128)(2,1)} %all_to_all.49) | data formatting | bytes 5242880 | tf_op jit(solution)/shard_map/all_to_all | solution.py:154
  293.7 31.7 %all-to-all-done.6 = bf16[16,256,432]{1,2,0:T(8,128)(2,1)} async-done(((bf16[16,256,432]{1,2,0:T(8,128)(2,1)}), bf16[16,256,432]{1,2,0:T(8,128)(2,1)}, u32[]{:S(2)}, u32[]{:S(2)}) %all-to-all-start.6) | async-done | bytes 3538976 | tf_op jit(solution)/shard_map/all_to_all | solution.py:60
  325.4 5.2 %all-to-all-start.5 = ((bf16[256,16,320]{0,2,1:T(8,128)(2,1)}), bf16[256,16,320]{0,2,1:T(8,128)(2,1)}, u32[]{:S(2)}, u32[]{:S(2)}) async-start(bf16[256,16,320]{0,2,1:T(8,128)(2,1)} %copy.138), calls=%async_computation.6 | async-start | bytes 5242880 | tf_op jit(solution)/shard_map/all_to_all | solution.py:154
  330.5 4.8 %fusion.99 = f32[8,2,16,432]{3,2,1,0:T(8,128)S(1)} fusion(bf16[8,2,16,5120]{3,2,1,0:T(8,128)(2,1)} %bitcast.10, bf16[5120,432,1,1]{1,0,3,2:T(8,128)(2,1)} %bitcast.42), kind=kOutput, calls=%fused_computation.106 | convolution fusion | flops 1132462080 | bytes 7487488 | tf_op jit(solution)/shard_map/dot_general | solution.py:36
  335.4 0.1 copy.132
  335.5 3.8 convolution_add_fusion.1
  339.4 0.2 fusion.87
  339.6 23.7 %all-to-all-done.5 = bf16[256,16,320]{0,2,1:T(8,128)(2,1)} async-done(((bf16[256,16,320]{0,2,1:T(8,128)(2,1)}), bf16[256,16,320]{0,2,1:T(8,128)(2,1)}, u32[]{:S(2)}, u32[]{:S(2)}) %all-to-all-start.5) | async-done | bytes 2621472 | tf_op jit(solution)/shard_map/all_to_all | solution.py:154
  363.3 2.2 stack.29
  365.5 5.2 %all-to-all-start.4 = ((bf16[16,1,2,128,432]{3,4,2,1,0:T(8,128)(2,1)}), bf16[16,1,2,128,432]{3,4,2,1,0:T(8,128)(2,1)}, u32[]{:S(2)}, u32[]{:S(2)}) async-start(bf16[16,1,2,128,432]{3,4,2,1,0:T(8,128)(2,1)} %stack.29), calls=%async_computation.5 | async-start | bytes 7077888 | tf_op jit(solution)/shard_map/all_to_all | solution.py:49
  370.9 1.3 fusion.67
  372.2 6.1 %copy.142 = bf16[16,256,432]{2,1,0:T(8,128)(2,1)} copy(bf16[16,256,432]{1,2,0:T(8,128)(2,1)} %all-to-all-done.6) | data formatting | bytes 7077888 | tf_op jit(solution)/shard_map/all_to_all | solution.py:60
  378.3 1.8 slice.39
  380.1 3.0 copy.149
  383.1 2.6 multiply_reduce_fusion
  386.4 1.3 collective-permute-start.1
  388.4 22.1 %collective-permute-start.2 = (f32[]{:T(128)}, f32[]{:T(128)}, u32[]{:S(2)}, u32[]{:S(2)}) collective-permute-start(f32[]{:T(128)} %add.106), channel_id=1, source_target_pairs={{0,32},{32,0},{1,33},{33,1},{2,34},{34,2},{3,35},{35,3},{4,36},{36... | collective-permute-start | bytes 20 | tf_op jit(solution)/shard_map/ppermute | solution.py:89
  410.5 1.6 collective-permute-done.2
  412.7 1.1 collective-permute-start.3
  413.8 1.4 collective-permute-done.3
  415.8 3.1 collective-permute-start.4
  418.9 0.8 collective-permute-done.4
  420.4 4.5 copy.139
  424.9 1.6 slice.38
  426.5 1.1 copy.148
  427.6 7.8 %all-to-all-start.3 = ((bf16[128,16,320]{0,2,1:T(8,128)(2,1)}), bf16[128,16,320]{0,2,1:T(8,128)(2,1)}, u32[]{:S(2)}, u32[]{:S(2)}) async-start(bf16[128,16,320]{0,2,1:T(8,128)(2,1)} %bitcast.12), calls=%async_computation.4 | async-start | bytes 2621440 | tf_op jit(solution)/shard_map/all_to_all | solution.py:146
  435.5 5.4 %fusion.25 = f32[320,432]{1,0:T(8,128)} fusion(f32[320,432]{1,0:T(8,128)} %get-tuple-element.21, bf16[16,256,432]{1,2,0:T(8,128)(2,1)} %all-to-all-done.6, bf16[256,16,320]{0,2,1:T(8,128)(2,1)} %all-to-all-done.5), kind=kOutput, calls=%fused_computation.28 | convolution fusion | flops 1132738560 | bytes 7266304 | tf_op jit(solution)/shard_map/dot_general | solution.py:40
  440.9 1.2 reduce_sum.29
  442.2 2.9 bitcast_add_fusion.1
  445.1 1.4 fusion.63
  446.5 2.2 fusion.96
  448.7 1.7 copy.136
  450.4 0.5 copy.137
  450.9 3.2 all-to-all-done.3
  454.1 2.8 fusion.46
  456.9 2.4 fusion.41
  459.4 2.7 add_divide_fusion
  (55 shorter events, 1.0 us)
Async XLA Ops:
  7.2 192.3 %copy-start = (bf16[128,5120]{1,0:T(8,128)(2,1)S(1)}, bf16[128,5120]{1,0:T(8,128)(2,1)}, u32[]{:S(2)}) copy-start(bf16[128,5120]{1,0:T(8,128)(2,1)} %param.12) | copy-start | bytes 3932164
  11.3 7.7 %copy-start.8 = (f32[432,320]{0,1:T(8,128)S(1)}, f32[432,320]{0,1:T(8,128)}, u32[]{:S(2)}) copy-start(f32[432,320]{0,1:T(8,128)} %param.15) | copy-start | bytes 1658884
  11.3 68.5 %all-to-all-start = ((bf16[16,320,432]{2,1,0:T(8,128)(2,1)}), bf16[16,320,432]{2,1,0:T(8,128)(2,1)}, u32[]{:S(2)}, u32[]{:S(2)}) async-start(bf16[16,320,432]{2,1,0:T(8,128)(2,1)} %stack.20), calls=%async_computation | async-start | bytes 10485760 | tf_op jit(solution)/shard_map/all_to_all | solution.py:49
  82.6 66.1 %all-to-all-start.1 = ((bf16[16,320,432]{2,1,0:T(8,128)(2,1)}), bf16[16,320,432]{2,1,0:T(8,128)(2,1)}, u32[]{:S(2)}, u32[]{:S(2)}) async-start(bf16[16,320,432]{2,1,0:T(8,128)(2,1)} %stack.22), calls=%async_computation.1 | async-start | bytes 10485760 | tf_op jit(solution)/shard_map/all_to_all | solution.py:49
  87.8 2.0 copy-start.4
  87.8 108.9 %reduce-scatter.2.cloned.1.call-start = ((), (), s32[]{:S(2)}) async-start(), calls=%async_computation.8 | async-start | bytes 2949120 | tf_op jit(solution)/shard_map/reduce_scatter | solution.py:143
  89.8 2.7 copy-start.5
  92.5 4.2 copy-start.9
  148.7 4.2 slice-start
  148.7 4.2 slice-start.1
  196.8 7.6 %collective-permute-start = (bf16[32,5120]{1,0:T(8,128)(2,1)}, bf16[32,5120]{1,0:T(8,128)(2,1)S(1)}, u32[]{:S(2)}, u32[]{:S(2)}) collective-permute-start(bf16[32,5120]{1,0:T(8,128)(2,1)} %reduce-scatter.2.cloned.1.call-done), channel_id=1, source_target_pairs={{0,1},{1,0},{2,3},{3,2},{4,5},{5,4},{6,7},{7,6},{8,9},{9,8},{10,11... | collective-permute-start | bytes 983048 | tf_op jit(solution)/shard_map/ppermute | solution.py:147
  207.4 60.9 %all-to-all-start.2 = ((bf16[8,32,5120]{2,1,0:T(8,128)(2,1)}), bf16[8,32,5120]{2,1,0:T(8,128)(2,1)}, u32[]{:S(2)}, u32[]{:S(2)}) async-start(bf16[8,32,5120]{2,1,0:T(8,128)(2,1)} %stack.24), calls=%async_computation.3 | async-start | bytes 5242880 | tf_op jit(solution)/shard_map/all_to_all | solution.py:49
  270.3 55.1 %all-to-all-start.6 = ((bf16[16,256,432]{1,2,0:T(8,128)(2,1)}), bf16[16,256,432]{1,2,0:T(8,128)(2,1)}, u32[]{:S(2)}, u32[]{:S(2)}) async-start(bf16[16,256,432]{1,2,0:T(8,128)(2,1)} %broadcast_in_dim.12), calls=%async_computation.7 | async-start | bytes 7077888 | tf_op jit(solution)/shard_map/all_to_all | solution.py:60
  325.4 37.9 %all-to-all-start.5 = ((bf16[256,16,320]{0,2,1:T(8,128)(2,1)}), bf16[256,16,320]{0,2,1:T(8,128)(2,1)}, u32[]{:S(2)}, u32[]{:S(2)}) async-start(bf16[256,16,320]{0,2,1:T(8,128)(2,1)} %copy.138), calls=%async_computation.6 | async-start | bytes 5242880 | tf_op jit(solution)/shard_map/all_to_all | solution.py:154
  365.5 62.1 %all-to-all-start.4 = ((bf16[16,1,2,128,432]{3,4,2,1,0:T(8,128)(2,1)}), bf16[16,1,2,128,432]{3,4,2,1,0:T(8,128)(2,1)}, u32[]{:S(2)}, u32[]{:S(2)}) async-start(bf16[16,1,2,128,432]{3,4,2,1,0:T(8,128)(2,1)} %stack.29), calls=%async_computation.5 | async-start | bytes 7077888 | tf_op jit(solution)/shard_map/all_to_all | solution.py:49
  386.4 1.4 collective-permute-start.1
  388.4 23.7 %collective-permute-start.2 = (f32[]{:T(128)}, f32[]{:T(128)}, u32[]{:S(2)}, u32[]{:S(2)}) collective-permute-start(f32[]{:T(128)} %add.106), channel_id=1, source_target_pairs={{0,32},{32,0},{1,33},{33,1},{2,34},{34,2},{3,35},{35,3},{4,36},{36... | collective-permute-start | bytes 20 | tf_op jit(solution)/shard_map/ppermute | solution.py:89
  412.7 2.5 collective-permute-start.3
  415.8 4.0 collective-permute-start.4
  427.6 26.5 %all-to-all-start.3 = ((bf16[128,16,320]{0,2,1:T(8,128)(2,1)}), bf16[128,16,320]{0,2,1:T(8,128)(2,1)}, u32[]{:S(2)}, u32[]{:S(2)}) async-start(bf16[128,16,320]{0,2,1:T(8,128)(2,1)} %bitcast.12), calls=%async_computation.4 | async-start | bytes 2621440 | tf_op jit(solution)/shard_map/all_to_all | solution.py:146
  435.5 6.7 %copy-start.2 = (bf16[128,1,16,432]{0,3,2,1:T(8,128)(2,1)S(1)}, bf16[128,1,16,432]{0,3,2,1:T(8,128)(2,1)}, u32[]{:S(2)}) copy-start(bf16[128,1,16,432]{0,3,2,1:T(8,128)(2,1)} %copy.149) | copy-start | bytes 5308420
  442.1 2.9 copy-start.3
  442.1 2.9 copy-start.6
  450.4 3.7 copy-start.10
  454.1 2.8 copy-start.7
  456.9 2.5 copy-start.12
  456.9 2.5 copy-start.11
  459.4 2.8 copy-start.1
Sparse Core Ops, SparseCore 0:
  156.2 40.5 reduce-scatter.1
